TPU v7x, 128 devices: a whole 4x4x4 slice. The times are simulated.
128 devices in a mesh: depth: 2 (over core), row: 16 (over z, x), col: 4 (over y).
Axes of the slice: x: 4, y: 4, z: 4, core: 2. Of those that a mesh axis runs over, the one named last changes fastest.
Arguments:
- right_side: bfloat16 [4, 16, 8, 128, 512], P(None, 'row', ('depth', 'col')), may hold values from -6 to 6
- inverse_diag: bfloat16 [4, 16, 8, 1, 128, 128], P(None, 'row', ('depth', 'col')), may hold values from -2 to 2.5, as said below
- coupling: bfloat16 [3, 16, 1024, 8, 2048], P(None, 'row', None, ('depth', 'col')), may hold values from -0.0625 to 0.0625
- pattern: int32 [3, 16, 8, 8, 16], P(None, 'row', None, ('depth', 'col')), may hold values 0 or 1
Outputs:
- forward_solution: bfloat16 [4, 16, 8, 128, 512], P(None, 'row', ('depth', 'col'))
- solution: bfloat16 [4, 16, 8, 128, 512], P(None, 'row', ('depth', 'col'))
Inputs may be any that keep to these rules, and one draw needn't show every extreme that they name: `inverse_diag`: each block is lower triangular with positive diagonal.
All inputs are finite; a program needn't handle non-finite values. No bound on the sum of `pattern` on one device may be relied on, other than what follows from the above.
Results may differ from a plain program's by a relative error of at most 0.025.
Values may be sent and summed in bfloat16 or wider, within the bound.
A program may use at most 128 MiB of HBM per device.

v0:
```python
import jax
import jax.numpy as jnp
from jax import lax
from jax.sharding import PartitionSpec as P


def apply_inverse(inverse, vector, transposed):
    blocks_in = vector.reshape(inverse.shape[0], inverse.shape[1], vector.shape[-1])
    einsum_form = "tji,tjn->tin" if transposed else "tij,tjn->tin"
    result = jnp.einsum(einsum_form, inverse, blocks_in, preferred_element_type=jnp.float32)
    return result.astype(jnp.bfloat16).reshape(vector.shape)


def lift_upward(masked, share_in):
    portion = lax.all_gather(share_in, "row", axis=0, tiled=True)
    span_rows = portion.shape[0] * portion.shape[2]
    return jnp.dot(
        masked, portion.reshape(span_rows, portion.shape[-1]), preferred_element_type=jnp.float32
    )


def carry_downward(masked, share_in):
    portion = lax.all_gather(share_in, ("depth", "col"), axis=1, tiled=True)
    span_rows = portion.shape[1] * portion.shape[2]
    return lax.dot_general(
        masked,
        portion.reshape(span_rows, portion.shape[-1]),
        (((0,), (0,)), ((), ())),
        preferred_element_type=jnp.float32,
    )


def forward_sum(partial_value, share_rows):
    blocks = partial_value.reshape(
        lax.axis_size(("depth", "col")), share_rows, partial_value.shape[-1]
    )
    summed = lax.psum(blocks.astype(jnp.bfloat16), ("depth", "col")).astype(jnp.float32)
    return lax.dynamic_index_in_dim(summed, lax.axis_index(("depth", "col")), 0, keepdims=False)


def backward_sum(partial_value, share_rows):
    blocks = partial_value.reshape(lax.axis_size("row"), share_rows, partial_value.shape[-1])
    summed = lax.psum(blocks.astype(jnp.bfloat16), "row").astype(jnp.float32)
    return lax.dynamic_index_in_dim(summed, lax.axis_index("row"), 0, keepdims=False)


def body(right_side, inverse_diag, coupling, pattern):
    levels = right_side.shape[0]
    share_rows = right_side.shape[3]
    rhs_cols = right_side.shape[4]
    block_width = inverse_diag.shape[-1]
    masked = []
    for pair_at in range(levels - 1):
        slab = coupling[pair_at, 0, :, 0, :]
        gate = pattern[pair_at, 0, :, 0, :].astype(jnp.bfloat16)
        shaped = (
            slab.reshape(gate.shape[0], block_width, gate.shape[1], block_width)
            * gate[:, None, :, None]
        )
        masked.append(shaped.reshape(slab.shape))
    panel_spans = [(0, rhs_cols)]
    fwd_levels = []
    for level_at in range(levels):
        pieces = []
        for panel_at, (col_first, col_last) in enumerate(panel_spans):
            source = right_side[level_at, 0, 0, :, col_first:col_last]
            if level_at == 0:
                residual = source
            else:
                partial_value = lift_upward(
                    masked[level_at - 1], fwd_levels[level_at - 1][panel_at][None, None]
                )
                residual = (
                    source.astype(jnp.float32) - forward_sum(partial_value, share_rows)
                ).astype(jnp.bfloat16)
            pieces.append(apply_inverse(inverse_diag[level_at, 0, 0], residual, False))
        fwd_levels.append(pieces)
    bwd_levels = [None] * levels
    for level_at in reversed(range(levels)):
        pieces = []
        panel_at = 0
        known_part = fwd_levels[level_at][panel_at]
        if level_at == levels - 1:
            residual = known_part
        else:
            partial_value = carry_downward(
                masked[level_at], bwd_levels[level_at + 1][panel_at][None, None]
            )
            residual = (
                known_part.astype(jnp.float32) - backward_sum(partial_value, share_rows)
            ).astype(jnp.bfloat16)
        pieces.append(apply_inverse(inverse_diag[level_at, 0, 0], residual, True))
        bwd_levels[level_at] = pieces
    forward_rows = []
    backward_rows = []
    for level_at in range(levels):
        forward_rows.append(jnp.concatenate(fwd_levels[level_at], axis=1))
        backward_rows.append(jnp.concatenate(bwd_levels[level_at], axis=1))
    forward_solution = jnp.stack(forward_rows).reshape(levels, 1, 1, share_rows, rhs_cols)
    solution = jnp.stack(backward_rows).reshape(levels, 1, 1, share_rows, rhs_cols)
    return (forward_solution, solution)


def solution(mesh):
    placed = (
        P(None, "row", ("depth", "col"), None, None),
        P(None, "row", ("depth", "col"), None, None, None),
        P(None, "row", None, ("depth", "col"), None),
        P(None, "row", None, ("depth", "col"), None),
    )
    return jax.shard_map(
        body,
        mesh=mesh,
        in_specs=placed,
        out_specs=(
            P(None, "row", ("depth", "col"), None, None),
            P(None, "row", ("depth", "col"), None, None),
        ),
        check_vma=False,
    )
```

profile of v0, /device:TPU:0, one launch (start us, length us, event | category | flops | bytes accessed | tf_op | source)
XLA Modules:
  0.0 735.9 jit_solution(18099699853977080136)
XLA Ops:
  7.2 0.0 all-gather.13.cloned.1.call-start
  7.2 1.8 convolution_convert_fusion.10
  9.0 0.0 all-gather.13.cloned.1.call-update
  9.0 0.0 all-reduce.7.cloned.1.call-start
  9.0 0.7 convert.11
  9.8 2.6 mul.62
  12.3 7.3 mul.63
  19.6 2.6 mul.71
  22.2 7.3 mul.72
  29.6 2.6 mul.67
  32.2 7.4 mul.68
  39.5 13.6 %slice_multiply_fusion.2 = (bf16[1,1,1024,1,2048]{4,2,3,1,0:T(8,128)(2,1)}, bf16[1,1,1024,1,2048]{4,2,3,1,0:T(8,128)(2,1)}, bf16[1,1,1024,1,2048]{4,2,3,1,0:T(8,128)(2,1)}) fusion(bf16[1,1,1024,1,2048]{4,2,3,1,0:T(8,128)(2,1)} %mul.63, bf16[3,1,1024,1,2048]{4,2,3,1,0:T(8,128)(2,1)} %param.6, bf16[1,1,1024,1,2048]{4,2,3,1,0:T(8,128)(2,1)} %mul.72, ...), kind=kLoop, calls=%fused_computation.8 | loop fusion | flops 6291456 | bytes 37748736 | tf_op jit(solution)/shard_map/mul | solution.py:57
  53.1 5.1 all-gather.13.cloned.1.call-done
  58.2 6.2 fusion.9
  64.5 0.0 all-reduce.7.cloned.1.call-update
  64.5 0.0 all-gather.15.cloned.1.call-start
  64.5 62.1 %all-reduce.7.cloned.1.call-done = bf16[8,128,512]{2,1,0:T(8,128)(2,1)} async-done(((bf16[8,128,512]{2,1,0:T(8,128)(2,1)}), bf16[8,128,512]{2,1,0:T(8,128)(2,1)}) %all-reduce.7.cloned.1.call-update) | async-done | bytes 1048592 | tf_op jit(solution)/shard_map/psum | solution.py:37
  126.6 1.7 convolution_convert_fusion.5
  128.4 0.0 all-gather.15.cloned.1.call-update
  128.4 0.0 all-reduce.9.cloned.1.call-start
  128.5 45.3 %all-gather.15.cloned.1.call-done = bf16[2048,512]{1,0:T(8,128)(2,1)} async-done(((bf16[128,512]{1,0:T(8,128)(2,1)}), bf16[2048,512]{1,0:T(8,128)(2,1)}) %all-gather.15.cloned.1.call-update) | async-done | bytes 2097168 | tf_op jit(solution)/shard_map/all_gather | solution.py:15
  173.7 6.2 fusion.12
  179.9 0.0 all-reduce.9.cloned.1.call-update
  180.0 0.0 all-gather.17.cloned.1.call-start
  180.0 62.1 %all-reduce.9.cloned.1.call-done = bf16[8,128,512]{2,1,0:T(8,128)(2,1)} async-done(((bf16[8,128,512]{2,1,0:T(8,128)(2,1)}), bf16[8,128,512]{2,1,0:T(8,128)(2,1)}) %all-reduce.9.cloned.1.call-update) | async-done | bytes 1048592 | tf_op jit(solution)/shard_map/psum | solution.py:37
  242.1 1.7 convolution_convert_fusion.4
  243.9 0.0 all-gather.17.cloned.1.call-update
  243.9 0.0 all-reduce.11.cloned.1.call-start
  243.9 44.5 %all-gather.17.cloned.1.call-done = bf16[2048,512]{1,0:T(8,128)(2,1)} async-done(((bf16[128,512]{1,0:T(8,128)(2,1)}), bf16[2048,512]{1,0:T(8,128)(2,1)}) %all-gather.17.cloned.1.call-update) | async-done | bytes 2097168 | tf_op jit(solution)/shard_map/all_gather | solution.py:15
  288.5 6.2 fusion.15
  294.7 0.0 all-reduce.11.cloned.1.call-update
  294.7 0.0 all-gather.19.cloned.1.call-start
  294.7 62.1 %all-reduce.11.cloned.1.call-done = bf16[8,128,512]{2,1,0:T(8,128)(2,1)} async-done(((bf16[8,128,512]{2,1,0:T(8,128)(2,1)}), bf16[8,128,512]{2,1,0:T(8,128)(2,1)}) %all-reduce.11.cloned.1.call-update) | async-done | bytes 1048592 | tf_op jit(solution)/shard_map/psum | solution.py:37
  356.8 1.1 convolution_convert_fusion.3
  357.9 0.9 convolution_convert_fusion.9
  358.8 0.0 all-gather.19.cloned.1.call-update
  358.8 0.2 all-reduce.13.cloned.1.call-start
  359.0 15.1 %fusion.2 = (bf16[2048,1024]{0,1:T(8,128)(2,1)}, bf16[2048,1024]{0,1:T(8,128)(2,1)}, bf16[2048,1024]{0,1:T(8,128)(2,1)}) fusion(bf16[128,8,16,128]{3,2,1,0:T(8,128)(2,1)} %bitcast.180, bf16[3,1,1024,1,2048]{4,2,3,1,0:T(8,128)(2,1)} %param.6, bf16[128,8,16,128]{3,2,1,0:T(8,128)(2,1)} %bitcast.182, bf16[128,8,16,128]{3,2,1,0:T(8,128)(2,1)} %bitcast.181), kind=kLoop, calls=%fused_computation.5 | loop fusion | flops 6291456 | bytes 37748736 | tf_op jit(solution)/shard_map/dot_general | solution.py:25
  374.1 6.4 copy.26
  380.5 1.1 all-gather.19.cloned.1.call-done
  381.6 6.3 convolution_convert_fusion.2
  387.9 0.0 all-gather.21.cloned.1.call-start
  387.9 92.3 %all-reduce.13.cloned.1.call-done = bf16[16,128,512]{2,1,0:T(8,128)(2,1)} async-done(((bf16[16,128,512]{2,1,0:T(8,128)(2,1)}), bf16[16,128,512]{2,1,0:T(8,128)(2,1)}) %all-reduce.13.cloned.1.call-update) | async-done | bytes 2097168 | tf_op jit(solution)/shard_map/psum | solution.py:43
  480.2 1.8 convolution_convert_fusion.8
  482.0 0.0 all-gather.21.cloned.1.call-update
  482.0 0.0 all-reduce.15.cloned.1.call-start
  482.1 6.4 copy.25
  488.5 16.4 %all-gather.21.cloned.1.call-done = bf16[1024,512]{0,1:T(8,128)(2,1)} async-done(((bf16[128,512]{0,1:T(8,128)(2,1)}), bf16[1024,512]{0,1:T(8,128)(2,1)}) %all-gather.21.cloned.1.call-update) | async-done | bytes 1048592 | tf_op jit(solution)/shard_map/all_gather | solution.py:23
  504.9 6.3 convolution_convert_fusion.1
  511.2 0.0 all-reduce.15.cloned.1.call-update
  511.2 0.0 all-gather.23.cloned.1.call-start
  511.2 92.3 %all-reduce.15.cloned.1.call-done = bf16[16,128,512]{2,1,0:T(8,128)(2,1)} async-done(((bf16[16,128,512]{2,1,0:T(8,128)(2,1)}), bf16[16,128,512]{2,1,0:T(8,128)(2,1)}) %all-reduce.15.cloned.1.call-update) | async-done | bytes 2097168 | tf_op jit(solution)/shard_map/psum | solution.py:43
  603.5 1.8 convolution_convert_fusion.7
  605.3 0.0 all-gather.23.cloned.1.call-update
  605.3 0.0 all-reduce.17.cloned.1.call-start
  605.3 6.4 copy.24
  611.7 16.4 %all-gather.23.cloned.1.call-done = bf16[1024,512]{0,1:T(8,128)(2,1)} async-done(((bf16[128,512]{0,1:T(8,128)(2,1)}), bf16[1024,512]{0,1:T(8,128)(2,1)}) %all-gather.23.cloned.1.call-update) | async-done | bytes 1048592 | tf_op jit(solution)/shard_map/all_gather | solution.py:23
  628.2 6.3 convolution_convert_fusion
  634.4 0.0 all-reduce.17.cloned.1.call-update
  634.5 0.9 maximum_bitcast_fusion
  635.3 91.5 %all-reduce.17.cloned.1.call-done = bf16[16,128,512]{2,1,0:T(8,128)(2,1)} async-done(((bf16[16,128,512]{2,1,0:T(8,128)(2,1)}), bf16[16,128,512]{2,1,0:T(8,128)(2,1)}) %all-reduce.17.cloned.1.call-update) | async-done | bytes 2097168 | tf_op jit(solution)/shard_map/psum | solution.py:43
  726.8 1.1 fusion.18
  728.0 0.1 maximum_bitcast_fusion.1
  728.1 1.0 copy.17
  (18 shorter events, 0.1 us)
Async XLA Ops:
  7.2 51.1 %all-gather.13.cloned.1.call-start = ((), (), s32[]{:S(2)}) async-start(), calls=%async_computation.6 | async-start | bytes 2228224 | tf_op jit(solution)/shard_map/all_gather | solution.py:15
  9.0 117.6 %all-reduce.7.cloned.1.call-start = ((), (), s32[]{:S(2)}) async-start(), calls=%async_computation | async-start | bytes 2097152 | tf_op jit(solution)/shard_map/psum | solution.py:37
  58.2 68.4 %copy-start.6 = (bf16[4,1,1,128,512]{4,3,2,1,0:T(8,128)(2,1)S(1)}, bf16[4,1,1,128,512]{4,3,2,1,0:T(8,128)(2,1)}, u32[]{:S(2)}) copy-start(bf16[4,1,1,128,512]{4,3,2,1,0:T(8,128)(2,1)} %param.4) | copy-start | bytes 1572868
  58.2 68.4 %copy-start.7 = (bf16[4,1,1,1,128,128]{5,4,3,2,1,0:T(8,128)(2,1)S(1)}, bf16[4,1,1,1,128,128]{5,4,3,2,1,0:T(8,128)(2,1)}, u32[]{:S(2)}) copy-start(bf16[4,1,1,1,128,128]{5,4,3,2,1,0:T(8,128)(2,1)} %param.5) | copy-start | bytes 393220
  64.5 109.2 %all-gather.15.cloned.1.call-start = ((), (), s32[]{:S(2)}) async-start(), calls=%async_computation.7 | async-start | bytes 2228224 | tf_op jit(solution)/shard_map/all_gather | solution.py:15
  128.4 113.7 %all-reduce.9.cloned.1.call-start = ((), (), s32[]{:S(2)}) async-start(), calls=%async_computation.1 | async-start | bytes 2097152 | tf_op jit(solution)/shard_map/psum | solution.py:37
  180.0 108.5 %all-gather.17.cloned.1.call-start = ((), (), s32[]{:S(2)}) async-start(), calls=%async_computation.8 | async-start | bytes 2228224 | tf_op jit(solution)/shard_map/all_gather | solution.py:15
  243.9 113.0 %all-reduce.11.cloned.1.call-start = ((), (), s32[]{:S(2)}) async-start(), calls=%async_computation.2 | async-start | bytes 2097152 | tf_op jit(solution)/shard_map/psum | solution.py:37
  294.7 86.9 %all-gather.19.cloned.1.call-start = ((), (), s32[]{:S(2)}) async-start(), calls=%async_computation.9 | async-start | bytes 1179648 | tf_op jit(solution)/shard_map/all_gather | solution.py:23
  358.8 121.4 %all-reduce.13.cloned.1.call-start = ((), (), s32[]{:S(2)}) async-start(), calls=%async_computation.3 | async-start | bytes 4194304 | tf_op jit(solution)/shard_map/psum | solution.py:43
  381.6 98.7 %copy-start.2 = (bf16[512,128]{0,1:T(8,128)(2,1)S(1)}, bf16[512,128]{0,1:T(8,128)(2,1)}, u32[]{:S(2)}) copy-start(bf16[512,128]{0,1:T(8,128)(2,1)} %convolution_convert_fusion.4) | copy-start | bytes 393220
  387.9 117.0 %all-gather.21.cloned.1.call-start = ((), (), s32[]{:S(2)}) async-start(), calls=%async_computation.10 | async-start | bytes 1179648 | tf_op jit(solution)/shard_map/all_gather | solution.py:23
  482.0 121.4 %all-reduce.15.cloned.1.call-start = ((), (), s32[]{:S(2)}) async-start(), calls=%async_computation.4 | async-start | bytes 4194304 | tf_op jit(solution)/shard_map/psum | solution.py:43
  504.9 98.6 %copy-start.1 = (bf16[512,128]{0,1:T(8,128)(2,1)S(1)}, bf16[512,128]{0,1:T(8,128)(2,1)}, u32[]{:S(2)}) copy-start(bf16[512,128]{0,1:T(8,128)(2,1)} %convolution_convert_fusion.5) | copy-start | bytes 393220
  511.2 117.0 %all-gather.23.cloned.1.call-start = ((), (), s32[]{:S(2)}) async-start(), calls=%async_computation.11 | async-start | bytes 1179648 | tf_op jit(solution)/shard_map/all_gather | solution.py:23
  605.3 121.5 %all-reduce.17.cloned.1.call-start = ((), (), s32[]{:S(2)}) async-start(), calls=%async_computation.5 | async-start | bytes 4194304 | tf_op jit(solution)/shard_map/psum | solution.py:43
  628.1 6.3 copy-start
  628.1 99.8 %copy-start.3 = (bf16[512,128]{1,0:T(8,128)(2,1)S(1)}, bf16[512,128]{1,0:T(8,128)(2,1)}, u32[]{:S(2)}) copy-start(bf16[512,128]{1,0:T(8,128)(2,1)} %convolution_convert_fusion.9) | copy-start | bytes 393220
  628.1 99.8 %copy-start.4 = (bf16[512,128]{1,0:T(8,128)(2,1)S(1)}, bf16[512,128]{1,0:T(8,128)(2,1)}, u32[]{:S(2)}) copy-start(bf16[512,128]{1,0:T(8,128)(2,1)} %convolution_convert_fusion.8) | copy-start | bytes 393220
  628.2 99.8 %copy-start.5 = (bf16[512,128]{1,0:T(8,128)(2,1)S(1)}, bf16[512,128]{1,0:T(8,128)(2,1)}, u32[]{:S(2)}) copy-start(bf16[512,128]{1,0:T(8,128)(2,1)} %convolution_convert_fusion.7) | copy-start | bytes 393220
Sparse Core Ops, SparseCore 0:
  10.7 47.4 all-gather.12
  64.6 61.9 all-reduce.6
  129.4 44.3 all-gather.14
  180.1 61.9 all-reduce.8
  244.1 44.3 all-gather.16
  294.8 61.9 all-reduce.10
  358.9 22.6 all-gather.18
  388.0 92.1 all-reduce.12
  482.2 22.6 all-gather.20
  511.3 92.1 all-reduce.14
  605.4 22.6 all-gather.22
  634.6 92.1 all-reduce.16
where the time goes:
time: 737 us; the launch traced here: 736 us
  waiting for transfers between devices  591 us (80%)
  local copies, waits for them, and re-layouts  50 us (7%)
  matrix products  49.3 us (7%)
  other arithmetic  30.3 us (4%)
  between operations  14.3 us (2%)
    psum x3, waiting for transfers between devices, backward_sum(): summed = lax.psum(blocks.astype(jnp.bfloat16), 'row').astype(jnp.float32)  276 us
    psum x3, waiting for transfers between devices, forward_sum(): lax.psum(blocks.astype(jnp.bfloat16), ('depth', 'col')).astype(jnp.float32)  186 us
    all_gather x3, waiting for transfers between devices, lift_upward(): portion = lax.all_gather(share_in, 'row', axis=0, tiled=True)  94.9 us
    all_gather x3, waiting for transfers between devices, carry_downward(): portion = lax.all_gather(share_in, ('depth', 'col'), axis=1, tiled=True)  33.9 us
    mul x6, local copies, waits for them, and re-layouts, body(): slab.reshape(gate.shape[0], block_width, gate.shape[1], block_width)  29.7 us
    dot_general x3, local copies, waits for them, and re-layouts, carry_downward(): lax.dot_general(masked, portion.reshape(span_rows, portion.shape[-1]), ((...  19.2 us
    dot_general x3, matrix products, carry_downward(): lax.dot_general(masked, portion.reshape(span_rows, portion.shape[-1]), ((...  18.8 us
    dot_general x3, matrix products, lift_upward(): jnp.dot(masked, portion.reshape(span_rows, portion.shape[-1]), preferred_...  18.6 us
  transfers between devices with their start and end apart: 12, of which 12 were waited for; matrix products, arithmetic and copies ran while one was open for 11% of the time, Pallas kernels for 0%

commit v1 on v0

--- a/solution.py
+++ b/solution.py
@@ -12,7 +12,12 @@
 
 
 def lift_upward(masked, share_in):
-    portion = lax.all_gather(share_in, "row", axis=0, tiled=True)
+    ring = [share_in]
+    for hop in range(15):
+        ring.append(lax.ppermute(ring[-1], "row", [(dev, (dev + 1) % 16) for dev in range(16)]))
+    portion = jnp.roll(
+        jnp.concatenate(ring[::-1], axis=0), (lax.axis_index("row") + 1) * ring[0].shape[0], axis=0
+    )
     span_rows = portion.shape[0] * portion.shape[2]
     return jnp.dot(
         masked, portion.reshape(span_rows, portion.shape[-1]), preferred_element_type=jnp.float32

time: 737 us -> 1000 us (1.36)
  waiting for transfers between devices: 591 us -> 850 us
  matrix products: 49.3 us -> 38.6 us
    ppermute x0 -> x45, waiting for transfers between devices: none -> 362 us  [lift_upward(): lax.ppermute(ring[-1], 'row', [(dev, (dev + 1) % 16) for dev in range(16)])]
    all_gather x3 -> x0, waiting for transfers between devices: 94.9 us -> none  [lift_upward(): portion = lax.all_gather(share_in, 'row', axis=0, tiled=True)]
  transfers between devices with their start and end apart: 12 -> 54, of which waited for: 12 -> 52; matrix products, arithmetic and copies ran while one was open for 11% -> 8% of each run, Pallas kernels for 0% -> 0%
where the time goes in v1:
time: 1000 us; the launch traced here: 997 us
  waiting for transfers between devices  850 us (85%)
  local copies, waits for them, and re-layouts  54.8 us (5%)
  matrix products  38.6 us (4%)
  other arithmetic  32.4 us (3%)
  between operations  14.6 us (1%)
    ppermute x45, waiting for transfers between devices, lift_upward(): lax.ppermute(ring[-1], 'row', [(dev, (dev + 1) % 16) for dev in range(16)])  362 us
    psum x3, waiting for transfers between devices, backward_sum(): summed = lax.psum(blocks.astype(jnp.bfloat16), 'row').astype(jnp.float32)  276 us
    psum x3, waiting for transfers between devices, forward_sum(): lax.psum(blocks.astype(jnp.bfloat16), ('depth', 'col')).astype(jnp.float32)  178 us
    all_gather x3, waiting for transfers between devices, carry_downward(): portion = lax.all_gather(share_in, ('depth', 'col'), axis=1, tiled=True)  33.8 us
    mul x6, local copies, waits for them, and re-layouts, body(): slab.reshape(gate.shape[0], block_width, gate.shape[1], block_width)  29.8 us
  transfers between devices with their start and end apart: 54, of which 52 were waited for; matrix products, arithmetic and copies ran while one was open for 8% of the time, Pallas kernels for 0%

profile of v1, /device:TPU:0, one launch (start us, length us, event | category | flops | bytes accessed | tf_op | source)
XLA Modules:
  0.0 996.8 jit_solution(14982104631491592231)
XLA Ops:
  10.0 8.2 collective-permute-done
  18.2 8.3 collective-permute-done.1
  26.5 8.3 collective-permute-done.2
  34.8 8.3 collective-permute-done.3
  43.1 8.3 collective-permute-done.4
  51.4 8.9 collective-permute-done.5
  60.2 9.4 collective-permute-done.6
  69.6 8.5 collective-permute-done.7
  78.1 8.3 collective-permute-done.8
  86.4 8.3 collective-permute-done.9
  94.7 8.3 collective-permute-done.10
  103.0 8.3 collective-permute-done.11
  112.0 7.6 collective-permute-done.12
  122.2 7.3 mul.63
  132.1 7.3 mul.68
  142.0 7.3 mul.72
  149.8 13.4 %slice_multiply_fusion.2 = (bf16[1,1,1024,1,2048]{4,2,3,1,0:T(8,128)(2,1)}, bf16[1,1,1024,1,2048]{4,2,3,1,0:T(8,128)(2,1)}, bf16[1,1,1024,1,2048]{4,2,3,1,0:T(8,128)(2,1)}) fusion(bf16[1,1,1024,1,2048]{4,2,3,1,0:T(8,128)(2,1)} %mul.63, bf16[3,1,1024,1,2048]{4,2,3,1,0:T(8,128)(2,1)} %param.8, bf16[1,1,1024,1,2048]{4,2,3,1,0:T(8,128)(2,1)} %mul.72, ...), kind=kLoop, calls=%fused_computation.14 | loop fusion | flops 6291456 | bytes 37748736 | tf_op jit(solution)/shard_map/mul | solution.py:62
  165.7 3.3 convolution_convert_fusion.5
  169.2 65.4 %all-reduce.7.cloned.1.call-done = bf16[8,128,512]{2,1,0:T(8,128)(2,1)} async-done(((bf16[8,128,512]{2,1,0:T(8,128)(2,1)}), bf16[8,128,512]{2,1,0:T(8,128)(2,1)}) %all-reduce.7.cloned.1.call-update) | async-done | bytes 1048592 | tf_op jit(solution)/shard_map/psum | solution.py:42
  237.2 6.8 collective-permute-done.15
  244.0 8.3 collective-permute-done.16
  252.3 8.3 collective-permute-done.17
  260.6 9.1 collective-permute-done.18
  269.7 9.1 collective-permute-done.19
  278.8 8.3 collective-permute-done.20
  287.1 8.3 collective-permute-done.21
  295.4 8.3 collective-permute-done.22
  303.7 8.3 collective-permute-done.23
  312.0 8.6 collective-permute-done.24
  320.6 9.6 collective-permute-done.25
  330.2 8.8 collective-permute-done.26
  339.0 8.3 collective-permute-done.27
  347.3 8.3 collective-permute-done.28
  355.8 8.3 collective-permute-done.29
  366.5 3.3 convolution_convert_fusion.4
  369.9 56.4 %all-reduce.9.cloned.1.call-done = bf16[8,128,512]{2,1,0:T(8,128)(2,1)} async-done(((bf16[8,128,512]{2,1,0:T(8,128)(2,1)}), bf16[8,128,512]{2,1,0:T(8,128)(2,1)}) %all-reduce.9.cloned.1.call-update) | async-done | bytes 1048592 | tf_op jit(solution)/shard_map/psum | solution.py:42
  428.9 6.8 collective-permute-done.30
  435.8 8.3 collective-permute-done.31
  444.1 8.3 collective-permute-done.32
  452.3 9.1 collective-permute-done.33
  461.5 9.1 collective-permute-done.34
  470.6 8.3 collective-permute-done.35
  478.9 8.3 collective-permute-done.36
  487.2 8.3 collective-permute-done.37
  495.4 8.3 collective-permute-done.38
  503.7 8.6 collective-permute-done.39
  512.3 9.6 collective-permute-done.40
  522.0 8.8 collective-permute-done.41
  530.8 8.3 collective-permute-done.42
  539.0 8.3 collective-permute-done.43
  547.3 8.3 collective-permute-done.44
  561.5 56.4 %all-reduce.11.cloned.1.call-done = bf16[8,128,512]{2,1,0:T(8,128)(2,1)} async-done(((bf16[8,128,512]{2,1,0:T(8,128)(2,1)}), bf16[8,128,512]{2,1,0:T(8,128)(2,1)}) %all-reduce.11.cloned.1.call-update) | async-done | bytes 1048592 | tf_op jit(solution)/shard_map/psum | solution.py:42
  620.1 15.1 %fusion.2 = (bf16[2048,1024]{0,1:T(8,128)(2,1)}, bf16[2048,1024]{0,1:T(8,128)(2,1)}, bf16[2048,1024]{0,1:T(8,128)(2,1)}) fusion(bf16[128,8,16,128]{3,2,1,0:T(8,128)(2,1)} %bitcast.185, bf16[3,1,1024,1,2048]{4,2,3,1,0:T(8,128)(2,1)} %param.8, bf16[128,8,16,128]{3,2,1,0:T(8,128)(2,1)} %bitcast.186, bf16[128,8,16,128]{3,2,1,0:T(8,128)(2,1)} %bitcast.187), kind=kLoop, calls=%fused_computation.5 | loop fusion | flops 6291456 | bytes 37748736 | tf_op jit(solution)/shard_map/dot_general | solution.py:30
  635.2 6.4 copy.22
  642.7 6.2 convolution_convert_fusion.2
  649.0 92.3 %all-reduce.13.cloned.1.call-done = bf16[16,128,512]{2,1,0:T(8,128)(2,1)} async-done(((bf16[16,128,512]{2,1,0:T(8,128)(2,1)}), bf16[16,128,512]{2,1,0:T(8,128)(2,1)}) %all-reduce.13.cloned.1.call-update) | async-done | bytes 2097168 | tf_op jit(solution)/shard_map/psum | solution.py:48
  743.1 6.4 copy.21
  749.5 16.4 %all-gather.9.cloned.1.call-done = bf16[1024,512]{0,1:T(8,128)(2,1)} async-done(((bf16[128,512]{0,1:T(8,128)(2,1)}), bf16[1024,512]{0,1:T(8,128)(2,1)}) %all-gather.9.cloned.1.call-update) | async-done | bytes 1048592 | tf_op jit(solution)/shard_map/all_gather | solution.py:28
  765.9 6.2 convolution_convert_fusion.1
  772.2 92.3 %all-reduce.15.cloned.1.call-done = bf16[16,128,512]{2,1,0:T(8,128)(2,1)} async-done(((bf16[16,128,512]{2,1,0:T(8,128)(2,1)}), bf16[16,128,512]{2,1,0:T(8,128)(2,1)}) %all-reduce.15.cloned.1.call-update) | async-done | bytes 2097168 | tf_op jit(solution)/shard_map/psum | solution.py:48
  866.4 6.4 copy.20
  872.8 16.4 %all-gather.11.cloned.1.call-done = bf16[1024,512]{0,1:T(8,128)(2,1)} async-done(((bf16[128,512]{0,1:T(8,128)(2,1)}), bf16[1024,512]{0,1:T(8,128)(2,1)}) %all-gather.11.cloned.1.call-update) | async-done | bytes 1048592 | tf_op jit(solution)/shard_map/all_gather | solution.py:28
  889.2 6.2 convolution_convert_fusion
  896.3 91.5 %all-reduce.17.cloned.1.call-done = bf16[16,128,512]{2,1,0:T(8,128)(2,1)} async-done(((bf16[16,128,512]{2,1,0:T(8,128)(2,1)}), bf16[16,128,512]{2,1,0:T(8,128)(2,1)}) %all-reduce.17.cloned.1.call-update) | async-done | bytes 2097168 | tf_op jit(solution)/shard_map/psum | solution.py:48
  (150 shorter events, 38.0 us)
Async XLA Ops:
  7.2 227.4 %all-reduce.7.cloned.1.call-start = ((), (), s32[]{:S(2)}) async-start(), calls=%async_computation | async-start | bytes 2097152 | tf_op jit(solution)/shard_map/psum | solution.py:42
  8.3 9.9 collective-permute-start
  18.2 8.3 collective-permute-start.1
  26.5 8.3 collective-permute-start.2
  34.8 8.3 collective-permute-start.3
  43.1 8.3 collective-permute-start.4
  51.4 8.9 collective-permute-start.5
  60.2 9.4 collective-permute-start.6
  69.6 8.5 collective-permute-start.7
  78.1 8.3 collective-permute-start.8
  86.4 8.3 collective-permute-start.9
  94.7 8.3 collective-permute-start.10
  103.0 8.3 collective-permute-start.11
  111.3 8.3 collective-permute-start.12
  119.6 29.8 %collective-permute-start.13 = (bf16[1,1,128,512]{3,2,1,0:T(8,128)(2,1)S(1)}, bf16[1,1,128,512]{3,2,1,0:T(8,128)(2,1)S(1)}, u32[]{:S(2)}, u32[]{:S(2)}) collective-permute-start(bf16[1,1,128,512]{3,2,1,0:T(8,128)(2,1)S(1)} %collective-permute-done.12), channel_id=1, source_target_pairs={{0,4},{4,8},{8,12},{12,16},{16,20},{20,24},{24,28},{28,32},{32,36}... | collective-permute-start | bytes 393224 | tf_op jit(solution)/shard_map/ppermute | solution.py:17
  149.4 13.9 %collective-permute-start.14 = (bf16[1,1,128,512]{3,2,1,0:T(8,128)(2,1)S(1)}, bf16[1,1,128,512]{3,2,1,0:T(8,128)(2,1)S(1)}, u32[]{:S(2)}, u32[]{:S(2)}) collective-permute-start(bf16[1,1,128,512]{3,2,1,0:T(8,128)(2,1)S(1)} %collective-permute-done.13), channel_id=1, source_target_pairs={{0,4},{4,8},{8,12},{12,16},{16,20},{20,24},{24,28},{28,32},{32,36}... | collective-permute-start | bytes 393224 | tf_op jit(solution)/shard_map/ppermute | solution.py:17
  163.6 2.2 copy-start.2
  165.7 68.8 %copy-start.6 = (bf16[4,1,1,128,512]{4,3,2,1,0:T(8,128)(2,1)S(1)}, bf16[4,1,1,128,512]{4,3,2,1,0:T(8,128)(2,1)}, u32[]{:S(2)}) copy-start(bf16[4,1,1,128,512]{4,3,2,1,0:T(8,128)(2,1)} %param.6) | copy-start | bytes 1572868
  165.7 68.8 %copy-start.7 = (bf16[4,1,1,1,128,128]{5,4,3,2,1,0:T(8,128)(2,1)S(1)}, bf16[4,1,1,1,128,128]{5,4,3,2,1,0:T(8,128)(2,1)}, u32[]{:S(2)}) copy-start(bf16[4,1,1,1,128,128]{5,4,3,2,1,0:T(8,128)(2,1)} %param.7) | copy-start | bytes 393220
  169.1 257.2 %all-reduce.9.cloned.1.call-start = ((), (), s32[]{:S(2)}) async-start(), calls=%async_computation.1 | async-start | bytes 2097152 | tf_op jit(solution)/shard_map/psum | solution.py:42
  235.7 8.4 collective-permute-start.15
  244.0 8.3 collective-permute-start.16
  252.3 8.3 collective-permute-start.17
  260.6 9.1 collective-permute-start.18
  269.7 9.1 collective-permute-start.19
  278.8 8.3 collective-permute-start.20
  287.1 8.3 collective-permute-start.21
  295.4 8.3 collective-permute-start.22
  303.7 8.3 collective-permute-start.23
  312.0 8.6 collective-permute-start.24
  320.6 9.7 collective-permute-start.25
  330.2 8.8 collective-permute-start.26
  339.0 8.3 collective-permute-start.27
  347.3 8.3 collective-permute-start.28
  355.6 8.4 collective-permute-start.29
  364.3 2.2 copy-start.1
  369.9 248.0 %all-reduce.11.cloned.1.call-start = ((), (), s32[]{:S(2)}) async-start(), calls=%async_computation.2 | async-start | bytes 2097152 | tf_op jit(solution)/shard_map/psum | solution.py:42
  427.4 8.4 collective-permute-start.30
  435.8 8.3 collective-permute-start.31
  444.1 8.3 collective-permute-start.32
  452.3 9.1 collective-permute-start.33
  461.5 9.1 collective-permute-start.34
  470.6 8.3 collective-permute-start.35
  478.9 8.3 collective-permute-start.36
  487.2 8.3 collective-permute-start.37
  495.4 8.3 collective-permute-start.38
  503.7 8.6 collective-permute-start.39
  512.3 9.6 collective-permute-start.40
  522.0 8.8 collective-permute-start.41
  530.8 8.3 collective-permute-start.42
  539.0 8.3 collective-permute-start.43
  547.3 8.3 collective-permute-start.44
  555.9 2.2 copy-start
  561.4 81.2 %all-gather.7.cloned.1.call-start = ((), (), s32[]{:S(2)}) async-start(), calls=%async_computation.6 | async-start | bytes 1179648 | tf_op jit(solution)/shard_map/all_gather | solution.py:28
  619.9 121.4 %all-reduce.13.cloned.1.call-start = ((), (), s32[]{:S(2)}) async-start(), calls=%async_computation.3 | async-start | bytes 4194304 | tf_op jit(solution)/shard_map/psum | solution.py:48
  648.9 117.0 %all-gather.9.cloned.1.call-start = ((), (), s32[]{:S(2)}) async-start(), calls=%async_computation.7 | async-start | bytes 1179648 | tf_op jit(solution)/shard_map/all_gather | solution.py:28
  743.1 121.5 %all-reduce.15.cloned.1.call-start = ((), (), s32[]{:S(2)}) async-start(), calls=%async_computation.4 | async-start | bytes 4194304 | tf_op jit(solution)/shard_map/psum | solution.py:48
  772.2 117.0 %all-gather.11.cloned.1.call-start = ((), (), s32[]{:S(2)}) async-start(), calls=%async_computation.8 | async-start | bytes 1179648 | tf_op jit(solution)/shard_map/all_gather | solution.py:28
  866.4 121.5 %all-reduce.17.cloned.1.call-start = ((), (), s32[]{:S(2)}) async-start(), calls=%async_computation.5 | async-start | bytes 4194304 | tf_op jit(solution)/shard_map/psum | solution.py:48
  895.5 93.5 %copy-start.3 = (bf16[512,128]{1,0:T(8,128)(2,1)S(1)}, bf16[512,128]{1,0:T(8,128)(2,1)}, u32[]{:S(2)}) copy-start(bf16[512,128]{1,0:T(8,128)(2,1)} %convolution_convert_fusion.12) | copy-start | bytes 393220
  895.5 93.5 %copy-start.4 = (bf16[512,128]{1,0:T(8,128)(2,1)S(1)}, bf16[512,128]{1,0:T(8,128)(2,1)}, u32[]{:S(2)}) copy-start(bf16[512,128]{1,0:T(8,128)(2,1)} %convolution_convert_fusion.11) | copy-start | bytes 393220
  895.5 93.5 %copy-start.5 = (bf16[512,128]{1,0:T(8,128)(2,1)S(1)}, bf16[512,128]{1,0:T(8,128)(2,1)}, u32[]{:S(2)}) copy-start(bf16[512,128]{1,0:T(8,128)(2,1)} %convolution_convert_fusion.10) | copy-start | bytes 393220
Sparse Core Ops, SparseCore 0:
  169.2 65.2 all-reduce.6
  370.0 56.2 all-reduce.8
  561.6 56.2 all-reduce.10
  620.0 22.6 all-gather.6
  649.0 92.1 all-reduce.12
  743.2 22.6 all-gather.8
  772.3 92.1 all-reduce.14
  866.5 22.6 all-gather.10
  895.6 92.1 all-reduce.16
